TPU v7x, 256 devices: a 4x2x16 block of a 4x16x16 slice. The times are simulated.
256 devices in a mesh: grp: 2 (over y), theta: 64 (over z, x), phi: 2 (over core).
Axes of the slice: x: 4, y: 2, z: 16, core: 2. Of those that a mesh axis runs over, the one named last changes fastest.
The devices are a block of a 4x16x16 slice.
Arguments:
- maps: bfloat16 [8, 4096, 4096], P('grp', 'theta', 'phi'), parts along dimension 0, may hold values from -6 to 6
- deltas: bfloat16 [4096, 4, 4096], P('phi', None, 'theta'), may hold values from -1 to 1
- spin_rows: bfloat16 [4096, 2, 4], P('phi'), may hold values from -1 to 1
- ell_index: int32 [4], replicated, may hold values from 1024 to 2047
- owner_map: int32 [4096], replicated, may hold values from 0 to 4095, each once
- prior: float32 [4], replicated, may hold values from 0.3 to 3
Outputs:
- gradient: float32 [8, 2, 4096], P('grp', None, ('theta', 'phi')), parts along dimension 0
There are 2 independent parts, one for each index of `grp`. A program takes and returns all parts, laid end to end along the dimension named above; an argument that names none is the same for every part. Nothing has to cross between parts.
Inputs may be any that keep to these rules, and one draw needn't show every extreme that they name: `ell_index`: every selected degree is at least 1024; tables may repeat a degree. A permutation of the Fourier indices; slot s of deltas and of the output belongs to the frequency owner_map[s].
All inputs are finite; a program needn't handle non-finite values.
Results may differ from a plain program's by a relative error of at most 0.0003.
Values may be sent and summed in bfloat16 or wider, within the bound.
A program may use at most 128 MiB of HBM per device.

v0:
```python
import functools
import math

import jax
import jax.numpy as jnp
import numpy as np
from jax import lax
from jax.experimental import pallas as pl
from jax.experimental.pallas import tpu as pltpu
from jax.sharding import PartitionSpec as P

F32, BF16, I16 = jnp.float32, jnp.bfloat16, jnp.int16
MESH = pl.DeviceIdType.MESH
VMEM = pl.BlockSpec(memory_space=pltpu.VMEM)
SMEM = pl.BlockSpec(memory_space=pltpu.SMEM)
NT = (((1,), (1,)), ((), ()))
TN = (((0,), (0,)), ((), ()))
LANES = 128
SPLIT = 32
CODE_TOP = 32700.0
EXTRA = 2


def halves(table):
    high = table.astype(jnp.bfloat16)
    low = (table - high.astype(np.float64)).astype(jnp.bfloat16)
    return jnp.asarray(high), jnp.asarray(low)


def turn(product, modulus):
    angle = 2.0 * np.pi / modulus * np.mod(product, modulus)
    return np.cos(angle), np.sin(angle)


def tables():
    step = np.arange(SPLIT)
    lane = np.arange(LANES)
    cos_a, sin_a = turn(np.outer(step, step), SPLIT)
    spread = np.kron(np.concatenate([cos_a, sin_a]), np.eye(8))
    cos_t, sin_t = turn(np.outer(step, lane), SPLIT * LANES)
    row_turn = np.stack([np.repeat(cos_t, 8, 0), np.repeat(sin_t, 8, 0)])
    cos_b, sin_b = turn(np.outer(lane, lane), LANES)
    wide = np.concatenate([cos_b, sin_b], 1)
    same = np.kron(np.eye(2), np.ones((SPLIT, SPLIT)))
    fold = [np.tile(np.tile(part, (2, 2)) * same, (1, 2)) for part in (cos_a, -sin_a)]
    fold = np.concatenate(fold, 1)
    cos_k, sin_k = turn(np.outer(lane, step), SPLIT * LANES)
    slot_turn = np.stack([np.tile(cos_k, (1, 4)), np.tile(sin_k, (1, 4))])
    spread_h, spread_l = halves(spread)
    wide_h, wide_l = halves(wide)
    fold_h, fold_l = halves(fold)
    return dict(
        spread_h=spread_h,
        spread_l=spread_l,
        row_turn=jnp.asarray(row_turn, F32),
        wide_h=wide_h,
        wide_l=wide_l,
        fold=jnp.concatenate([fold_h, fold_h, fold_l]),
        slot_turn=jnp.asarray(slot_turn, F32),
    )


def split2(value):
    high = value.astype(BF16)
    return high, (value - high.astype(F32)).astype(BF16)


def mm(left, right, dims=(((1,), (0,)), ((), ()))):
    return lax.dot_general(left, right, dims, preferred_element_type=F32)


def mm3(left_h, left_l, right_h, right_l, dims=(((1,), (0,)), ((), ()))):
    return mm(left_h, right_h, dims) + mm(left_h, right_l, dims) + mm(left_l, right_h, dims)


def row_kernel(x_ref, sh_ref, sl_ref, tw_ref, wh_ref, wl_ref, pos_ref, o_ref, yh_ref, yl_ref, rt_ref):
    cos_t, sin_t = tw_ref[0], tw_ref[1]

    def columns(z, i):
        return jnp.concatenate([z[8 * i : 8 * i + 8, LANES * a : LANES * (a + 1)] for a in range(SPLIT)], 0)

    def put(h, field, re_parts, im_parts):
        turned = []
        for re, im in zip(re_parts, im_parts):
            turned.append((re * cos_t + im * sin_t, im * cos_t - re * sin_t))
        for k1 in range(SPLIT):
            cut = slice(8 * k1, 8 * k1 + 8)
            re = jnp.concatenate([turned[0][0][cut], turned[1][0][cut]], 0)
            im = jnp.concatenate([turned[0][1][cut], turned[1][1][cut]], 0)
            re_h, re_l = split2(re)
            im_h, im_l = split2(im)
            top = pl.ds(k1 * LANES + field * SPLIT + 16 * h, 16)
            low = pl.ds(k1 * LANES + 64 + field * SPLIT + 16 * h, 16)
            yh_ref[top, :LANES] = re_h
            yh_ref[top, LANES:] = im_h
            yh_ref[low, :LANES] = im_h
            yh_ref[low, LANES:] = -re_h
            yl_ref[top, :LANES] = re_l
            yl_ref[top, LANES:] = im_l
            yl_ref[low, :LANES] = im_l
            yl_ref[low, LANES:] = -re_l

    for h in range(2):
        rows = pl.ds(16 * h, 16)
        v0, v1, v2, v3 = (x_ref[plane, rows, :].astype(F32) for plane in range(4))
        flat = jnp.concatenate([columns(v0, 0), columns(v0, 1)], 1).astype(BF16)
        out = mm(sh_ref[...], flat) + mm(sl_ref[...], flat)
        put(h, 0, [out[:256, :LANES], out[:256, LANES:]], [-out[256:, :LANES], -out[256:, LANES:]])
        q_re, q_im = v1 * v2, v1 * v3
        re_parts, im_parts = [], []
        for i in range(2):
            q_h, q_l = split2(jnp.concatenate([columns(q_re, i), columns(q_im, i)], 1))
            out = mm3(sh_ref[...], sl_ref[...], q_h, q_l)
            re_parts.append(out[:256, :LANES] + out[256:, LANES:])
            im_parts.append(out[:256, LANES:] - out[256:, :LANES])
        put(h, 1, re_parts, im_parts)

    def second(step, top):
        rows = pl.ds(pl.multiple_of(step * 256, 256), 256)
        out = mm3(wh_ref[...], wl_ref[...], yh_ref[rows, :], yl_ref[rows, :], NT)
        rt_ref[pl.ds(pl.multiple_of(step * 256, 256), LANES), :] = out[:, :LANES]
        rt_ref[pl.ds(pl.multiple_of(step * 256 + LANES, LANES), LANES), :] = out[:, LANES:]
        size = jnp.maximum(jnp.abs(out[:, :LANES]), jnp.abs(out[:, LANES:]))
        return jnp.maximum(top, jnp.max(size.reshape(16, 8, LANES), 0))

    top = lax.fori_loop(0, SPLIT // 2, second, jnp.zeros((8, LANES), F32))
    top = jnp.max(top, 0, keepdims=True)
    level = jnp.ceil(jnp.log2(jnp.maximum(top, 1e-30)) * 16.0 + 0.01)
    shrink = jnp.exp2(level * (-1.0 / 16.0))
    share = pos_ref.shape[0] // o_ref.shape[0]
    mark = jnp.broadcast_to(level, (EXTRA, LANES)).astype(jnp.int32).astype(I16)

    def gather(dest, _):
        for part in range(share // 16):
            base = dest * share + part * 16
            rows = [rt_ref[pl.ds(pos_ref[base + i], 1), :] for i in range(16)]
            x = jnp.concatenate(rows, 0)
            code = jnp.sqrt(jnp.abs(x) * shrink) * CODE_TOP + 0.5
            code = jnp.where(x < 0.0, -code, code).astype(jnp.int32)
            o_ref[dest, 16 * part : 16 * part + 16, :] = code.astype(I16)
        o_ref[dest, share : share + EXTRA, :] = mark
        return 0

    lax.fori_loop(0, o_ref.shape[0], gather, 0)


def row_stage(rows, position, n, share, t):
    length = rows.shape[2]
    return pl.pallas_call(
        row_kernel,
        out_shape=jax.ShapeDtypeStruct((n, share + EXTRA, LANES), I16),
        in_specs=[VMEM] * 6 + [SMEM],
        out_specs=VMEM,
        scratch_shapes=[
            pltpu.VMEM((length, 2 * LANES), BF16),
            pltpu.VMEM((length, 2 * LANES), BF16),
            pltpu.VMEM((length, LANES), F32),
        ],
        compiler_params=pltpu.CompilerParams(vmem_limit_bytes=56 * 2**20),
        name="row_stage",
    )(rows, t["spread_h"], t["spread_l"], t["row_turn"], t["wide_h"], t["wide_l"], position)


def column_kernel(
    n, send_ref, tab_ref, w_ref, hot_ref, fold_ref, st_ref, wh_ref, wl_ref, sum_ref,
    o_ref, recv_ref, t_ref, ure_ref, uim_ref, d_ref, acc_ref, ssem, rsem, lsem, share,
):
    theta, phi = lax.axis_index("theta"), lax.axis_index("phi")
    phis = lax.axis_size("phi")
    me = theta * phis + phi

    def peer(i):
        j = lax.rem(me + i, n)
        return j, {"theta": j // phis, "phi": lax.rem(j, phis)}

    barrier = pltpu.get_barrier_semaphore()

    def greet(i, _):
        pl.semaphore_signal(barrier, inc=1, device_id=peer(i)[1], device_id_type=MESH)
        return 0

    lax.fori_loop(1, n, greet, 0)
    pl.semaphore_wait(barrier, n - 1)
    own = pltpu.make_async_copy(send_ref.at[me], recv_ref.at[me], lsem)
    own.start()

    def launch(i, _):
        j, where = peer(i)
        pltpu.make_async_remote_copy(
            src_ref=send_ref.at[j],
            dst_ref=recv_ref.at[me],
            send_sem=ssem,
            recv_sem=rsem,
            device_id=where,
            device_id_type=MESH,
        ).start()
        return 0

    lax.fori_loop(1, n, launch, 0)

    def weigh(step, _):
        rows = pl.ds(pl.multiple_of(step * 512, 512), 512)
        w = mm(w_ref[rows, :], hot_ref[...])
        tab = tab_ref[rows, :].astype(F32)
        t_ref[0, rows, :] = tab * w[:, :LANES]
        t_ref[1, rows, :] = tab * w[:, LANES:]
        return 0

    lax.fori_loop(0, tab_ref.shape[0] // 512, weigh, 0)

    def fold(kl, _):
        t = jnp.concatenate([t_ref[f, pl.ds(kl, SPLIT, stride=LANES), :] for f in range(2)], 0)
        t_h, t_l = split2(t)
        v = mm(jnp.concatenate([t_h, t_l, t_h], 0), fold_ref[...], TN)
        v_re, v_im = v[:, :LANES], v[:, LANES:]
        c, s = st_ref[0, pl.ds(kl, 1), :], st_ref[1, pl.ds(kl, 1), :]
        ure_ref[pl.ds(kl, LANES, stride=LANES), :] = v_re * c + v_im * s
        uim_ref[pl.ds(kl, LANES, stride=LANES), :] = v_im * c - v_re * s
        return 0

    lax.fori_loop(0, LANES, fold, 0)

    own.wait()
    rest = pl.ds(0, n - 1)
    whole = pltpu.make_async_remote_copy(
        src_ref=send_ref.at[rest],
        dst_ref=recv_ref.at[rest],
        send_sem=ssem,
        recv_sem=rsem,
        device_id=peer(1)[1],
        device_id_type=MESH,
    )
    whole.wait_send()
    whole.wait_recv()

    def widen(tau, _):
        code = recv_ref[tau, :share, :].astype(jnp.int32).astype(F32)
        level = recv_ref[tau, share : share + EXTRA, :].astype(jnp.int32).astype(F32)[:1, :]
        grow = jnp.exp2(level * (1.0 / 16.0)) * (1.0 / CODE_TOP**2)
        d_ref[pl.ds(pl.multiple_of(tau * share, share), share), :] = code * jnp.abs(code) * grow
        return 0

    lax.fori_loop(0, n, widen, 0)
    sign = jnp.where(lax.broadcasted_iota(jnp.int32, (1, LANES), 1) < 64, 1.0, -1.0).astype(F32)

    def column(pair, _):
        cols = [d_ref[pl.ds(2 * pair + i, n, stride=share), :] for i in range(2)]
        d = jnp.concatenate(cols, 1)
        e = jnp.concatenate([pltpu.roll(x, 64, 1) * sign for x in cols], 1)
        r_h, r_l = split2(jnp.concatenate([d, e], 0))
        y = mm3(wh_ref[...], wl_ref[...], r_h, r_l)
        for i in range(2):
            y_s = y[:, i * LANES : (i + 1) * LANES]
            for j in range(4):
                row = j * share + 2 * pair + i
                rows = pl.ds(pl.multiple_of(row * LANES, LANES), LANES)
                acc_ref[pl.ds(row, 1), :] = jnp.sum(y_s * ure_ref[rows, :], 0, keepdims=True)
                acc_ref[pl.ds(LANES + row, 1), :] = jnp.sum(y_s * uim_ref[rows, :], 0, keepdims=True)
        return 0

    lax.fori_loop(0, share // 2, column, 0)
    a_h, a_m = split2(acc_ref[...])
    a_l = (acc_ref[...] - a_h.astype(F32) - a_m.astype(F32)).astype(BF16)
    o_ref[...] = mm(a_h, sum_ref[...]) + mm(a_m, sum_ref[...]) + mm(a_l, sum_ref[...])


def column_stage(send, tab, weights, t):
    n, share = send.shape[0], send.shape[1] - EXTRA
    length = tab.shape[0]
    hot = np.kron(np.eye(8), np.ones((1, share)))
    gather = np.zeros((LANES, LANES))
    gather[np.arange(LANES), np.arange(LANES) // SPLIT] = 1.0
    return pl.pallas_call(
        lambda *refs: column_kernel(n, *refs, share),
        out_shape=jax.ShapeDtypeStruct((2 * LANES, LANES), F32),
        in_specs=[VMEM] * 9,
        out_specs=VMEM,
        scratch_shapes=[
            pltpu.VMEM(send.shape, I16),
            pltpu.VMEM((2, length, LANES), F32),
            pltpu.VMEM((LANES * LANES, LANES), F32),
            pltpu.VMEM((LANES * LANES, LANES), F32),
            pltpu.VMEM((length, LANES), F32),
            pltpu.VMEM((2 * LANES, LANES), F32),
            pltpu.SemaphoreType.DMA,
            pltpu.SemaphoreType.DMA,
            pltpu.SemaphoreType.DMA,
        ],
        compiler_params=pltpu.CompilerParams(
            collective_id=0, has_side_effects=True, vmem_limit_bytes=56 * 2**20
        ),
        name="column_stage",
    )(
        send,
        tab,
        weights,
        jnp.asarray(hot, BF16),
        t["fold"],
        t["slot_turn"],
        t["wide_h"],
        t["wide_l"],
        jnp.asarray(gather, BF16),
    )


def on_device(maps, deltas, spin_rows, ell_index, owner_map, prior):
    t = tables()
    thetas, phis = lax.axis_size("theta"), lax.axis_size("phi")
    theta, phi = lax.axis_index("theta"), lax.axis_index("phi")
    length = maps.shape[2] * phis
    n = thetas * phis
    degrees = deltas.shape[1]
    share = deltas.shape[2] // phis
    rows = lax.all_to_all(maps, "phi", split_axis=1, concat_axis=2, tiled=True)
    position = (owner_map % SPLIT) * LANES + owner_map // SPLIT
    send = row_stage(rows, position, n, share, t)

    cut = deltas.reshape(deltas.shape[0], degrees, phis, share).transpose(2, 0, 1, 3)
    cut = cut.reshape(phis * deltas.shape[0], degrees * share)
    tab = lax.all_to_all(cut, "phi", split_axis=0, concat_axis=0, tiled=True)
    spins = lax.all_gather(spin_rows, "phi", axis=0, tiled=True)
    place = jnp.arange(length, dtype=jnp.int32)
    freq = jnp.where(place < length // 2, place, place - length)
    keep = jnp.abs(freq)[:, None, None] <= ell_index[None, None, :]
    weights = jnp.where(keep, spins, 0).astype(BF16).reshape(length, 2 * degrees)
    sums = column_stage(send, tab, weights, t)

    sums = sums[:, :4].reshape(2, degrees, share, 4).transpose(0, 3, 1, 2)
    scalar_real, scalar_imag = sums[0, 0] - sums[1, 2], sums[0, 2] + sums[1, 0]
    spin_real, spin_imag = sums[0, 1] - sums[1, 3], sums[0, 3] + sums[1, 1]
    ids = lax.dynamic_slice_in_dim(owner_map, (theta * phis + phi) * share, share)
    slot_freq = jnp.where(ids < length // 2, ids, ids - length)
    ell = ell_index.astype(F32)
    weight = 2.0 * math.pi / length * jnp.sqrt((2.0 * ell + 1.0) / (4.0 * math.pi)) / length
    keep = jnp.where(jnp.abs(slot_freq)[None, :] <= ell_index[:, None], weight[:, None], 0.0)
    coupling = (prior * jnp.sqrt(ell * (ell + 1.0)) / (length // 2))[:, None]
    inner_real = (-spin_imag - coupling * scalar_real) * keep
    inner_imag = (spin_real - coupling * scalar_imag) * keep
    turns = jnp.mod(-slot_freq, 4)
    phase_real = jnp.where(turns == 0, 1.0, jnp.where(turns == 2, -1.0, 0.0)).astype(F32)[None, :]
    phase_imag = jnp.where(turns == 1, 1.0, jnp.where(turns == 3, -1.0, 0.0)).astype(F32)[None, :]
    out_real = phase_real * inner_real - phase_imag * inner_imag
    out_imag = phase_real * inner_imag + phase_imag * inner_real
    return jnp.stack([out_real, out_imag], axis=1)


def solution(mesh):
    placed = (
        P("grp", "theta", "phi"),
        P("phi", None, "theta"),
        P("phi", None, None),
        P(),
        P(),
        P(),
    )
    return jax.shard_map(
        on_device,
        mesh=mesh,
        in_specs=placed,
        out_specs=P("grp", None, ("theta", "phi")),
        check_vma=False,
    )
```

profile of v0, /device:TPU:33, one launch (start us, length us, event | category | flops | bytes accessed | tf_op | source)
XLA Modules:
  0.0 134.0 jit_solution(11192042214087525055)
XLA Ops:
  0.0 3.0 %copy.33 = bf16[4,64,2048]{2,0,1:T(4,128)(2,1)} copy(bf16[4,64,2048]{2,1,0:T(8,128)(2,1)} %param.16) | data formatting | bytes 2097152 | tf_op args[0]
  3.0 24.1 %all-to-all-start = ((bf16[4,64,2048]{2,0,1:T(4,128)(2,1)}), bf16[4,64,2048]{2,0,1:T(4,128)(2,1)S(1)}, u32[]{:S(2)}, u32[]{:S(2)}) async-start(bf16[4,64,2048]{2,0,1:T(4,128)(2,1)} %copy.33), calls=%async_computation | async-start | bytes 2097152 | tf_op jit(solution)/shard_map/all_to_all | solution.py:314
  27.1 0.0 copy-done.2
  27.1 0.6 fusion.1.pos_ref
  27.8 0.1 compare_select_fusion.7
  27.9 1.0 copy.35
  28.9 0.0 all-to-all-done
  28.9 4.0 %all-to-all-start.1 = ((bf16[2,2048,128]{1,2,0:T(8,128)(2,1)}), bf16[2,2048,128]{1,2,0:T(8,128)(2,1)S(1)}, u32[]{:S(2)}, u32[]{:S(2)}) async-start(bf16[2,2048,128]{1,2,0:T(8,128)(2,1)} %bitcast.4), calls=%async_computation.1 | async-start | bytes 2097152 | tf_op jit(solution)/shard_map/all_to_all | solution.py:320
  32.8 1.1 copy.41
  33.9 0.0 copy-start.1
  33.9 0.0 copy-start.3
  34.0 0.0 copy-start.4
  34.0 1.6 %all_to_all.23.x_ref = bf16[4,32,4096]{2,1,0:T(8,128)(2,1)} reshape(bf16[4,32,2,2048]{3,2,1,0:T(2,128)(2,1)S(1)} %bitcast.44) | data formatting | bytes 2097152 | tf_op jit(solution)/shard_map/all_to_all | solution.py:314
  35.6 1.9 %all_gather.3 = bf16[4096,2,4]{0,2,1:T(4,128)(2,1)S(1)} all-gather(bf16[2048,2,4]{0,2,1:T(4,128)(2,1)S(1)} %copy-done.1), channel_id=1, replica_groups=mesh['grp'=2,'theta'=64,'phi'=2] {'phi'}, dimensions={0}, use_global_device_ids=true | all-gather | bytes 98304 | tf_op jit(solution)/shard_map/all_gather | solution.py:321
  37.4 0.0 copy-done.3
  37.5 0.1 broadcast_compare_fusion
  37.6 1.3 %copy.37.refs_2_ = bf16[4096,8]{1,0:T(8,128)(2,1)} copy(bf16[4096,8]{0,1:T(8,128)(2,1)S(1)} %reshape.438) | data formatting | bytes 131072 | tf_op jit(solution)/shard_map/reshape | solution.py:325
  39.0 14.6 %row_stage.1.refs_0_ = s16[128,34,128]{2,1,0:T(8,128)(2,1)} custom-call(bf16[4,32,4096]{2,1,0:T(8,128)(2,1)} %all_to_all.23.x_ref, bf16[512,256]{1,0:T(8,128)(2,1)} %constant.111.clone.sh_ref, bf16[512,256]{1,0:T(8,128)(2,1)} %constant.112.clone.sl_ref, f32[2,256,128]{2,1,0:T(8,128)} %constant.117.clone.tw_ref, ...), custom_call_target="tpu_custom_call" | custom-call | tf_op jit(solution)/shard_map/row_stage/pallas_call | solution.py:149
  53.6 0.0 all-to-all-done.1
  53.6 1.3 copy.36
  54.9 77.4 %column_stage.1 = f32[256,128]{1,0:T(8,128)} custom-call(s16[128,34,128]{2,1,0:T(8,128)(2,1)} %row_stage.1.refs_0_, bf16[4096,128]{1,0:T(8,128)(2,1)} %bitcast.42, bf16[4096,8]{1,0:T(8,128)(2,1)} %copy.37.refs_2_, bf16[8,256]{1,0:T(8,128)(2,1)} %constant.119.clone.refs_3_, bf16[192,256]{1,0:T(8,128)(2,1)} %constant.121.refs_4_, ...), custom_call_target="tpu_custom_call" | custom-call | tf_op jit(solution)/shard_map/column_stage/pallas_call | solution.py:273
  132.3 1.0 copy.38
  133.3 0.1 multiply_subtract_fusion
  133.4 0.6 copy.39
  (13 shorter events, 0.1 us)
Async XLA Ops:
  3.0 24.1 %copy-start.2 = (s32[4096]{0:T(1024)S(1)}, s32[4096]{0:T(1024)}, u32[]{:S(2)}) copy-start(s32[4096]{0:T(1024)} %param.20) | copy-start | bytes 49156
  3.0 24.9 %copy-start = (bf16[2048,4,64]{0,2,1:T(8,128)(2,1)S(1)}, bf16[2048,4,64]{0,2,1:T(8,128)(2,1)}, u32[]{:S(2)}) copy-start(bf16[2048,4,64]{0,2,1:T(8,128)(2,1)} %param.17) | copy-start | bytes 3145732
  3.0 25.9 %all-to-all-start = ((bf16[4,64,2048]{2,0,1:T(4,128)(2,1)}), bf16[4,64,2048]{2,0,1:T(4,128)(2,1)S(1)}, u32[]{:S(2)}, u32[]{:S(2)}) async-start(bf16[4,64,2048]{2,0,1:T(4,128)(2,1)} %copy.33), calls=%async_computation | async-start | bytes 2097152 | tf_op jit(solution)/shard_map/all_to_all | solution.py:314
  28.9 24.7 %all-to-all-start.1 = ((bf16[2,2048,128]{1,2,0:T(8,128)(2,1)}), bf16[2,2048,128]{1,2,0:T(8,128)(2,1)S(1)}, u32[]{:S(2)}, u32[]{:S(2)}) async-start(bf16[2,2048,128]{1,2,0:T(8,128)(2,1)} %bitcast.4), calls=%async_computation.1 | async-start | bytes 2097152 | tf_op jit(solution)/shard_map/all_to_all | solution.py:320
  33.9 1.6 %copy-start.1 = (bf16[2048,2,4]{0,2,1:T(4,128)(2,1)S(1)}, bf16[2048,2,4]{0,2,1:T(4,128)(2,1)}, u32[]{:S(2)}) copy-start(bf16[2048,2,4]{0,2,1:T(4,128)(2,1)} %param.18) | copy-start | bytes 98308
  33.9 3.5 %copy-start.3 = (s32[4]{0:T(128)S(1)}, s32[4]{0:T(128)}, u32[]{:S(2)}) copy-start(s32[4]{0:T(128)} %param.19) | copy-start | bytes 52
  34.0 3.5 %copy-start.4 = (f32[4]{0:T(128)S(1)}, f32[4]{0:T(128)}, u32[]{:S(2)}) copy-start(f32[4]{0:T(128)} %param.21) | copy-start | bytes 52
where the time goes:
time: 134 us
  Pallas kernels  92 us (69%)
  starting transfers between devices  28.1 us (21%)
  local copies, waits for them, and re-layouts  11 us (8%)
  blocking collectives  1.87 us (1%)
    pallas_call x1, Pallas kernels, column_stage(): pl.pallas_call(lambda *refs: column_kernel(n, *refs, share), out_shape=ja...  77.4 us
    all_to_all x1, starting transfers between devices, on_device(): rows = lax.all_to_all(maps, 'phi', split_axis=1, concat_axis=2, tiled=True)  24.1 us
    pallas_call x1, Pallas kernels, row_stage(): pl.pallas_call(row_kernel, out_shape=jax.ShapeDtypeStruct((n, share + EXT...  14.6 us
    all_to_all x1, starting transfers between devices, on_device(): tab = lax.all_to_all(cut, 'phi', split_axis=0, concat_axis=0, tiled=True)  3.95 us
    unnamed x11, local copies, waits for them, and re-layouts  3.03 us
    all_to_all x2, local copies, waits for them, and re-layouts, on_device(): rows = lax.all_to_all(maps, 'phi', split_axis=1, concat_axis=2, tiled=True)  2.68 us
  transfers between devices with their start and end apart: 2, of which 0 were waited for; matrix products, arithmetic and copies ran while one was open for 3% of the time, Pallas kernels for 11%

commit v1 on v0

v1 whole, which is shorter than its diff:
```python
import math

import jax
import jax.numpy as jnp
import numpy as np
from jax import lax
from jax.experimental import pallas as pl
from jax.experimental.pallas import tpu as pltpu
from jax.sharding import PartitionSpec as P

F32, BF16, I16 = jnp.float32, jnp.bfloat16, jnp.int16
MESH = pl.DeviceIdType.MESH
VMEM = pl.BlockSpec(memory_space=pltpu.VMEM)
SMEM = pl.BlockSpec(memory_space=pltpu.SMEM)
ANY = pl.BlockSpec(memory_space=pl.ANY)
NN = (((1,), (0,)), ((), ()))
NT = (((1,), (1,)), ((), ()))
TN = (((0,), (0,)), ((), ()))
LANES = 128
SPLIT = 32
HALF = LANES // 2
GROUP = 32
CODE_TOP = 32700.0


def halves(table):
    high = table.astype(jnp.bfloat16)
    low = (table - high.astype(np.float64)).astype(jnp.bfloat16)
    return jnp.asarray(high), jnp.asarray(low)


def turn(product, modulus):
    angle = 2.0 * np.pi / modulus * np.mod(product, modulus)
    return np.cos(angle), np.sin(angle)


def tables():
    step = np.arange(SPLIT)
    lane = np.arange(LANES)
    cos_a, sin_a = turn(np.outer(step, step), SPLIT)
    spread_h, spread_l = halves(np.kron(np.concatenate([cos_a, sin_a]), np.eye(8)))
    cos_t, sin_t = turn(np.outer(step, lane), SPLIT * LANES)
    row_turn = np.stack([np.repeat(cos_t, 8, 0), np.repeat(sin_t, 8, 0)])
    cos_b, sin_b = turn(np.outer(lane, lane), LANES)
    wide = np.concatenate([cos_b, sin_b], 1)
    wide_h, wide_l = halves(wide)
    fold_h, fold_l = halves(np.concatenate([np.kron(np.eye(2), cos_a), np.kron(np.eye(2), -sin_a)], 1))
    cos_k, sin_k = turn(np.outer(lane, step), SPLIT * LANES)
    slot_turn = np.stack([np.tile(cos_k, (1, 4)), np.concatenate([sin_k, sin_k, -sin_k, -sin_k], 1)])
    gather = np.zeros((LANES, LANES))
    gather[lane, lane // SPLIT] = 1.0
    return (
        spread_h,
        spread_l,
        jnp.asarray(row_turn, F32),
        wide_h,
        wide_l,
        jnp.asarray(wide, F32),
        jnp.concatenate([fold_h, fold_h, fold_l]),
        jnp.asarray(slot_turn, F32),
        jnp.asarray(gather, BF16),
    )


def split2(value):
    high = value.astype(BF16)
    return high, (value - high.astype(F32)).astype(BF16)


def mm(left, right, dims=NN):
    return lax.dot_general(left, right, dims, preferred_element_type=F32)


def mm3(left_h, left_l, right_h, right_l, dims=NN):
    return mm(left_h, right_h, dims) + mm(left_h, right_l, dims) + mm(left_l, right_h, dims)


def row_spectra(x_ref, sh_ref, sl_ref, tw_ref, wh_ref, wl_ref, yh_ref, yl_ref, rt_ref):
    cos_t, sin_t = tw_ref[0], tw_ref[1]

    def columns(z, i):
        return jnp.concatenate([z[8 * i : 8 * i + 8, LANES * a : LANES * (a + 1)] for a in range(SPLIT)], 0)

    def put(h, field, re_parts, im_parts):
        turned = []
        for re, im in zip(re_parts, im_parts):
            turned.append((re * cos_t + im * sin_t, im * cos_t - re * sin_t))
        for k1 in range(SPLIT):
            cut = slice(8 * k1, 8 * k1 + 8)
            re = jnp.concatenate([turned[0][0][cut], turned[1][0][cut]], 0)
            im = jnp.concatenate([turned[0][1][cut], turned[1][1][cut]], 0)
            re_h, re_l = split2(re)
            im_h, im_l = split2(im)
            top = pl.ds(k1 * LANES + field * SPLIT + 16 * h, 16)
            low = pl.ds(k1 * LANES + HALF + field * SPLIT + 16 * h, 16)
            yh_ref[top, :LANES] = re_h
            yh_ref[top, LANES:] = im_h
            yh_ref[low, :LANES] = im_h
            yh_ref[low, LANES:] = -re_h
            yl_ref[top, :LANES] = re_l
            yl_ref[top, LANES:] = im_l
            yl_ref[low, :LANES] = im_l
            yl_ref[low, LANES:] = -re_l

    row_id = lax.broadcasted_iota(jnp.int32, (16, LANES), 0)
    lane_id = lax.broadcasted_iota(jnp.int32, (16, LANES), 1)
    bound = jnp.zeros((1, LANES), F32)
    for h in range(2):
        rows = pl.ds(16 * h, 16)
        v0, v1, v2, v3 = (x_ref[plane, rows, :].astype(F32) for plane in range(4))
        q_re, q_im = v1 * v2, v1 * v3
        sizes = jnp.sum(jnp.abs(v0), 1, keepdims=True), jnp.sum(jnp.abs(q_re) + jnp.abs(q_im), 1, keepdims=True)
        for field in range(2):
            here = lane_id % HALF == row_id + (field * SPLIT + 16 * h)
            bound = bound + jnp.sum(jnp.where(here, sizes[field], 0.0), 0, keepdims=True)
        flat = jnp.concatenate([columns(v0, 0), columns(v0, 1)], 1).astype(BF16)
        out = mm(sh_ref[...], flat) + mm(sl_ref[...], flat)
        put(h, 0, [out[:256, :LANES], out[:256, LANES:]], [-out[256:, :LANES], -out[256:, LANES:]])
        re_parts, im_parts = [], []
        for i in range(2):
            q_h, q_l = split2(jnp.concatenate([columns(q_re, i), columns(q_im, i)], 1))
            out = mm3(sh_ref[...], sl_ref[...], q_h, q_l)
            re_parts.append(out[:256, :LANES] + out[256:, LANES:])
            im_parts.append(out[:256, LANES:] - out[256:, :LANES])
        put(h, 1, re_parts, im_parts)

    def second(step, _):
        rows = pl.ds(pl.multiple_of(step * 256, 256), 256)
        out = mm3(wh_ref[...], wl_ref[...], yh_ref[rows, :], yl_ref[rows, :], NT)
        rt_ref[pl.ds(pl.multiple_of(step * 256, 256), LANES), :] = out[:, :LANES]
        rt_ref[pl.ds(pl.multiple_of(step * 256 + LANES, LANES), LANES), :] = out[:, LANES:]
        return 0

    lax.fori_loop(0, SPLIT // 2, second, 0)
    return jnp.maximum(bound, 1e-30)


def kernel(
    maps_ref, delta_ref, spin_ref, pos_ref, sh_ref, sl_ref, tw_ref, wh_ref, wl_ref, wide_ref, fold_ref, st_ref, sum_ref,
    o_ref,
    x_ref, yh_ref, yl_ref, rt_ref, send_ref, recv_ref, bound_ref, bounds_ref, tab_ref, w_ref, t_ref, wt_ref,
    mine_ref, h_ref, d_ref, acc_ref, near_sem, far_sem, out_sem, ssem, rsem, bsem, brsem,
):
    theta, phi = lax.axis_index("theta"), lax.axis_index("phi")
    phis = lax.axis_size("phi")
    n, share = recv_ref.shape[0], recv_ref.shape[1]
    me = theta * phis + phi
    other = phis - 1 - phi
    half = maps_ref.shape[2]
    here = pl.ds(pl.multiple_of(phi * half, half), half)

    def peer(i):
        j = lax.rem(me + i, n)
        return j, {"theta": j // phis, "phi": lax.rem(j, phis)}

    def cut(whose):
        return pl.ds(pl.multiple_of(whose * share, share), share)

    pieces = (
        (lambda whose: maps_ref.at[:, cut(whose), :], x_ref.at[:, :, here]),
        (lambda whose: delta_ref.at[:, cut(whose), :], tab_ref.at[:, :, here]),
        (lambda whose: spin_ref, w_ref.at[:, here]),
    )
    near = [pltpu.make_async_copy(src(phi), dst, near_sem.at[k]) for k, (src, dst) in enumerate(pieces)]
    far = [
        pltpu.make_async_remote_copy(
            src_ref=src(other),
            dst_ref=dst,
            send_sem=out_sem.at[k],
            recv_sem=far_sem.at[k],
            device_id={"phi": other},
            device_id_type=MESH,
        )
        for k, (src, dst) in enumerate(pieces)
    ]
    near[0].start()

    barrier = pltpu.get_barrier_semaphore()

    def greet(i, _):
        pl.semaphore_signal(barrier, inc=1, device_id=peer(i)[1], device_id_type=MESH)
        return 0

    lax.fori_loop(1, n, greet, 0)
    pl.semaphore_wait(barrier, n - 1)
    for copy in far:
        copy.start()
    for copy in near[1:]:
        copy.start()
    near[0].wait()
    far[0].wait()

    bound = row_spectra(x_ref, sh_ref, sl_ref, tw_ref, wh_ref, wl_ref, yh_ref, yl_ref, rt_ref)
    bound_ref[...] = bound
    bounds_ref[0] = bound
    shrink = 1.0 / bound

    def tell(i):
        return pltpu.make_async_remote_copy(
            src_ref=bound_ref,
            dst_ref=bounds_ref.at[i],
            send_sem=bsem,
            recv_sem=brsem,
            device_id=peer(i)[1],
            device_id_type=MESH,
        )

    def encoded(dest, target, slot):
        for part in range(share // 16):
            base = dest * share + part * 16
            rows = [rt_ref[pl.ds(pos_ref[base + i], 1), :] for i in range(16)]
            x = jnp.concatenate(rows, 0)
            code = jnp.sqrt(jnp.abs(x) * shrink) * CODE_TOP + 0.5
            code = jnp.where(x < 0.0, -code, code).astype(jnp.int32)
            target[slot, 16 * part : 16 * part + 16, :] = code.astype(I16)

    def post(i):
        pltpu.make_async_remote_copy(
            src_ref=send_ref.at[i],
            dst_ref=recv_ref.at[i],
            send_sem=ssem,
            recv_sem=rsem.at[i // GROUP],
            device_id=peer(i)[1],
            device_id_type=MESH,
        ).start()

    def tell_all(i, _):
        tell(i).start()
        return 0

    lax.fori_loop(1, n, tell_all, 0)
    encoded(peer(1)[0], send_ref, 1)

    def ship(i, _):
        post(i - 1)
        encoded(peer(i)[0], send_ref, i)
        return 0

    lax.fori_loop(2, n, ship, 0)
    encoded(me, recv_ref, 0)
    post(n - 1)

    for copy in near[1:]:
        copy.wait()
    for copy in far[1:]:
        copy.wait()
    degrees = tab_ref.shape[0]

    def arrange(kh, _):
        lanes = pl.ds(pl.multiple_of(kh * LANES, LANES), LANES)
        for j in range(degrees):
            rows = pl.ds(pl.multiple_of(kh * LANES + j * share, share), share)
            t_ref[rows, :] = tab_ref[j, :, lanes].astype(F32)
        wt_ref[pl.ds(pl.multiple_of(kh * 8, 8), 8), :] = w_ref[:, lanes]
        return 0

    lax.fori_loop(0, SPLIT, arrange, 0)

    def order(i, _):
        mine_ref[pl.ds(i, 1), :] = wide_ref[pl.ds(lax.rem(me - i + n, n), 1), :]
        return 0

    lax.fori_loop(0, n, order, 0)
    lane_id = lax.broadcasted_iota(jnp.int32, (1, LANES), 1)
    first = lane_id < HALF
    sign = jnp.where(first, 1.0, -1.0).astype(F32)

    def fold(pair, _):
        tops = []
        for i in range(2):
            js = 2 * pair + i
            j = js // share
            t = t_ref[pl.ds(js, SPLIT, stride=LANES), :]
            both = [t * wt_ref[pl.ds(f * degrees + j, SPLIT, stride=8), :] for f in range(2)]
            t_h, t_l = split2(jnp.concatenate(both, 0))
            v = mm(jnp.concatenate([t_h, t_l, t_h], 0), fold_ref[...], TN)
            tops.append(v * st_ref[0] + pltpu.roll(v, HALF, 1) * st_ref[1])
        lows = [pltpu.roll(u, HALF, 1) * sign for u in tops]
        r_h, r_l = split2(jnp.concatenate([jnp.concatenate(tops, 1), jnp.concatenate(lows, 1)], 0))
        m_h, m_l = split2(mine_ref[...])
        out = mm3(m_h, m_l, r_h, r_l)
        for i in range(2):
            g = out[:, i * LANES : (i + 1) * LANES]
            back = pltpu.roll(g, HALF, 1)
            rows = pl.ds(pl.multiple_of((2 * pair + i) * LANES, LANES), LANES)
            h_ref[rows, :LANES] = jnp.where(first, g, back)
            h_ref[rows, LANES:] = jnp.where(first, back, g)
        return 0

    lax.fori_loop(0, LANES // 2, fold, 0)
    acc_ref[...] = jnp.zeros_like(acc_ref)

    rest = pl.ds(1, n - 1)
    bounds = pltpu.make_async_remote_copy(
        src_ref=bounds_ref.at[rest],
        dst_ref=bounds_ref.at[rest],
        send_sem=bsem,
        recv_sem=brsem,
        device_id=peer(1)[1],
        device_id_type=MESH,
    )
    bounds.wait_send()
    bounds.wait_recv()
    for group in range(n // GROUP):
        begin = group * GROUP
        part = pl.ds(max(begin, 1), GROUP - (begin == 0))
        pltpu.make_async_remote_copy(
            src_ref=send_ref.at[part],
            dst_ref=recv_ref.at[part],
            send_sem=ssem,
            recv_sem=rsem.at[group],
            device_id=peer(1)[1],
            device_id_type=MESH,
        ).wait_recv()

        def widen(k, _):
            slot = begin + k
            code = recv_ref[slot].astype(jnp.int32).astype(F32)
            grow = bounds_ref[slot] * (1.0 / CODE_TOP**2)
            d_ref[pl.ds(pl.multiple_of(k * share, share), share), :] = code * jnp.abs(code) * grow
            return 0

        lax.fori_loop(0, GROUP, widen, 0)

        def gain(s, _):
            d = d_ref[pl.ds(s, GROUP, stride=share), :]
            for j in range(degrees):
                row = j * share + s
                rows = pl.ds(pl.multiple_of(row * LANES + begin, GROUP), GROUP)
                for k in range(2):
                    sums = jnp.sum((d * h_ref[rows, k * LANES : (k + 1) * LANES]).reshape(-1, 8, LANES), 0)
                    place = pl.ds(pl.multiple_of((k * LANES + row) * 8, 8), 8)
                    acc_ref[place, :] = acc_ref[place, :] + sums
            return 0

        lax.fori_loop(0, share, gain, 0)

    total = jnp.sum(acc_ref[...].reshape(2 * LANES, 8, LANES), 1)
    a_h, a_m = split2(total)
    a_l = (total - a_h.astype(F32) - a_m.astype(F32)).astype(BF16)
    o_ref[...] = mm(a_h, sum_ref[...]) + mm(a_m, sum_ref[...]) + mm(a_l, sum_ref[...])
    sent = pl.ds(1, n - 1)
    pltpu.make_async_remote_copy(
        src_ref=send_ref.at[sent],
        dst_ref=recv_ref.at[sent],
        send_sem=ssem,
        recv_sem=rsem.at[0],
        device_id=peer(1)[1],
        device_id_type=MESH,
    ).wait_send()


def sums_of(maps, deltas, spins, position, n):
    degrees, slots, half = deltas.shape
    share = slots * half // position.shape[0]
    length = position.shape[0]
    dma = pltpu.SemaphoreType.DMA
    return pl.pallas_call(
        kernel,
        out_shape=jax.ShapeDtypeStruct((2 * LANES, LANES), F32),
        in_specs=[ANY] * 3 + [SMEM] + [VMEM] * 9,
        out_specs=VMEM,
        scratch_shapes=[
            pltpu.VMEM((4, SPLIT, length), BF16),
            pltpu.VMEM((length, 2 * LANES), BF16),
            pltpu.VMEM((length, 2 * LANES), BF16),
            pltpu.VMEM((length, LANES), F32),
            pltpu.VMEM((n, share, LANES), I16),
            pltpu.VMEM((n, share, LANES), I16),
            pltpu.VMEM((1, LANES), F32),
            pltpu.VMEM((n, 1, LANES), F32),
            pltpu.VMEM((degrees, share, length), BF16),
            pltpu.VMEM((2 * degrees, length), F32),
            pltpu.VMEM((length, LANES), F32),
            pltpu.VMEM((SPLIT * 2 * degrees, LANES), F32),
            pltpu.VMEM((n, 2 * LANES), F32),
            pltpu.VMEM((LANES * LANES, 2 * LANES), F32),
            pltpu.VMEM((GROUP * share, LANES), F32),
            pltpu.VMEM((2 * LANES * 8, LANES), F32),
            dma((3,)),
            dma((3,)),
            dma((3,)),
            dma,
            dma((n // GROUP,)),
            dma,
            dma,
        ],
        compiler_params=pltpu.CompilerParams(
            collective_id=0, has_side_effects=True, vmem_limit_bytes=56 * 2**20
        ),
        name="coefficient_sums",
    )(maps, deltas, spins, position, *tables())


def on_device(maps, deltas, spin_rows, ell_index, owner_map, prior):
    thetas, phis = lax.axis_size("theta"), lax.axis_size("phi")
    theta, phi = lax.axis_index("theta"), lax.axis_index("phi")
    half = maps.shape[2]
    length = half * phis
    n = thetas * phis
    degrees = deltas.shape[1]
    share = deltas.shape[2] // phis
    position = (owner_map % SPLIT) * LANES + owner_map // SPLIT
    place = phi * half + jnp.arange(half, dtype=jnp.int32)
    freq = jnp.where(place < length // 2, place, place - length)
    keep = jnp.abs(freq)[None, None, :] <= ell_index[None, :, None]
    spins = jnp.where(keep, spin_rows.transpose(1, 2, 0).astype(F32), 0.0).reshape(2 * degrees, half)
    sums = sums_of(maps, deltas.transpose(1, 2, 0), spins, position, n)

    sums = sums[:, :4].reshape(2, degrees, share, 4).transpose(0, 3, 1, 2)
    scalar_real, scalar_imag = sums[0, 0] - sums[1, 2], sums[0, 2] + sums[1, 0]
    spin_real, spin_imag = sums[0, 1] - sums[1, 3], sums[0, 3] + sums[1, 1]
    ids = lax.dynamic_slice_in_dim(owner_map, (theta * phis + phi) * share, share)
    slot_freq = jnp.where(ids < length // 2, ids, ids - length)
    ell = ell_index.astype(F32)
    weight = 2.0 * math.pi / length * jnp.sqrt((2.0 * ell + 1.0) / (4.0 * math.pi)) / length
    keep = jnp.where(jnp.abs(slot_freq)[None, :] <= ell_index[:, None], weight[:, None], 0.0)
    coupling = (prior * jnp.sqrt(ell * (ell + 1.0)) / (length // 2))[:, None]
    inner_real = (-spin_imag - coupling * scalar_real) * keep
    inner_imag = (spin_real - coupling * scalar_imag) * keep
    turns = jnp.mod(-slot_freq, 4)
    phase_real = jnp.where(turns == 0, 1.0, jnp.where(turns == 2, -1.0, 0.0)).astype(F32)[None, :]
    phase_imag = jnp.where(turns == 1, 1.0, jnp.where(turns == 3, -1.0, 0.0)).astype(F32)[None, :]
    out_real = phase_real * inner_real - phase_imag * inner_imag
    out_imag = phase_real * inner_imag + phase_imag * inner_real
    return jnp.stack([out_real, out_imag], axis=1)


def solution(mesh):
    placed = (
        P("grp", "theta", "phi"),
        P("phi", None, "theta"),
        P("phi", None, None),
        P(),
        P(),
        P(),
    )
    return jax.shard_map(
        on_device,
        mesh=mesh,
        in_specs=placed,
        out_specs=P("grp", None, ("theta", "phi")),
        check_vma=False,
    )
```

time: 134 us -> 109 us (0.81)
  starting transfers between devices: 28.1 us -> 0 us
  Pallas kernels: 92 us -> 104 us
  local copies, waits for them, and re-layouts: 11 us -> 3.65 us
  blocking collectives: 1.87 us -> 0 us
    all_to_all x2 -> x0, starting transfers between devices: 28.1 us -> none  [the longest x1 24.1 us: on_device(): rows = lax.all_to_all(maps, 'phi', split_axis=1, concat_axis=2, tiled=True)]
    pallas_call x2 -> x1, Pallas kernels: 92 us -> 104 us  [sums_of(): pl.pallas_call(kernel, out_shape=jax.ShapeDtypeStruct((2 * LANES, LANES),...]
    all_to_all x3 -> x0, local copies, waits for them, and re-layouts: 3.98 us -> none  [the longest x2 2.68 us: on_device(): rows = lax.all_to_all(maps, 'phi', split_axis=1, concat_axis=2, tiled=True)]
    all_gather x1 -> x0, blocking collectives: 1.87 us -> none  [on_device(): spins = lax.all_gather(spin_rows, 'phi', axis=0, tiled=True)]
    unnamed x11 -> x8, local copies, waits for them, and re-layouts: 3.03 us -> 1.4 us
  transfers between devices with their start and end apart: 2 -> 0, of which waited for: 0 -> 0; matrix products, arithmetic and copies ran while one was open for 3% -> 0% of each run, Pallas kernels for 11% -> 0%
where the time goes in v1:
time: 109 us
  Pallas kernels  104 us (95%)
  local copies, waits for them, and re-layouts  3.65 us (3%)
  other arithmetic  1.58 us (1%)
    pallas_call x1, Pallas kernels, sums_of(): pl.pallas_call(kernel, out_shape=jax.ShapeDtypeStruct((2 * LANES, LANES),...  104 us

profile of v1, /device:TPU:33, one launch (start us, length us, event | category | flops | bytes accessed | tf_op | source)
XLA Modules:
  0.0 108.9 jit_solution(5475673986096010999)
XLA Ops:
  0.0 0.0 copy-start.1
  0.0 0.0 copy-start
  0.0 0.7 copy-done.1
  0.7 0.1 compare_select_fusion.7
  0.8 0.7 broadcast_compare_fusion
  1.6 0.0 copy-done
  1.6 0.6 reshape.431.spin_ref
  2.3 0.6 fusion.1.pos_ref
  2.9 103.6 %coefficient_sums.1 = f32[256,128]{1,0:T(8,128)} custom-call(bf16[4,64,2048]{2,1,0:T(8,128)(2,1)} %maps_ref.1, bf16[4,64,2048]{2,1,0:T(8,128)(2,1)} %bitcast.34, f32[8,2048]{1,0:T(8,128)} %reshape.431.spin_ref, s32[4096]{0:T(1024)} %fusion.1.pos_ref, bf16[512,256]{1,0:T(8,128)(2,1)} %constant.110.clone.sh_ref, bf16[512,256]{1,0:T(8,128)(2,1)} %constant.111.clone.sl_ref, ...), custom_call_target="tpu_custom_call" | custom-call | tf_op jit(solution)/shard_map/coefficient_sums/pallas_call | solution.py:358
  106.5 1.0 copy.17
  107.5 0.0 copy-start.2
  107.5 0.0 copy-start.3
  107.5 0.7 copy-done.2
  108.2 0.0 copy-done.3
  108.2 0.1 multiply_subtract_fusion
  108.3 0.6 copy.18
  (7 shorter events, 0.1 us)
Async XLA Ops:
  0.0 0.7 copy-start.1
  0.0 1.6 %copy-start = (bf16[2048,2,4]{0,2,1:T(4,128)(2,1)S(1)}, bf16[2048,2,4]{0,2,1:T(4,128)(2,1)}, u32[]{:S(2)}) copy-start(bf16[2048,2,4]{0,2,1:T(4,128)(2,1)} %param.18) | copy-start | bytes 98308
  107.5 0.7 copy-start.2
  107.5 0.7 copy-start.3

commit v2 on v1

--- a/solution.py
+++ b/solution.py
@@ -20,6 +20,7 @@
 SPLIT = 32
 HALF = LANES // 2
 GROUP = 32
+UNROLL = 2
 CODE_TOP = 32700.0
 
 
@@ -47,8 +48,8 @@
     fold_h, fold_l = halves(np.concatenate([np.kron(np.eye(2), cos_a), np.kron(np.eye(2), -sin_a)], 1))
     cos_k, sin_k = turn(np.outer(lane, step), SPLIT * LANES)
     slot_turn = np.stack([np.tile(cos_k, (1, 4)), np.concatenate([sin_k, sin_k, -sin_k, -sin_k], 1)])
-    gather = np.zeros((LANES, LANES))
-    gather[lane, lane // SPLIT] = 1.0
+    gather = np.zeros((8, LANES))
+    gather[lane // SPLIT, lane] = 1.0
     return (
         spread_h,
         spread_l,
@@ -136,7 +137,7 @@
 
 
 def kernel(
-    maps_ref, delta_ref, spin_ref, pos_ref, sh_ref, sl_ref, tw_ref, wh_ref, wl_ref, wide_ref, fold_ref, st_ref, sum_ref,
+    maps_ref, delta_ref, spin_ref, pos_ref, ell_ref, sh_ref, sl_ref, tw_ref, wh_ref, wl_ref, wide_ref, fold_ref, st_ref, sum_ref,
     o_ref,
     x_ref, yh_ref, yl_ref, rt_ref, send_ref, recv_ref, bound_ref, bounds_ref, tab_ref, w_ref, t_ref, wt_ref,
     mine_ref, h_ref, d_ref, acc_ref, near_sem, far_sem, out_sem, ssem, rsem, bsem, brsem,
@@ -151,7 +152,7 @@
 
     def peer(i):
         j = lax.rem(me + i, n)
-        return j, {"theta": j // phis, "phi": lax.rem(j, phis)}
+        return j, {"theta": lax.div(j, phis), "phi": lax.rem(j, phis)}
 
     def cut(whose):
         return pl.ds(pl.multiple_of(whose * share, share), share)
@@ -159,7 +160,7 @@
     pieces = (
         (lambda whose: maps_ref.at[:, cut(whose), :], x_ref.at[:, :, here]),
         (lambda whose: delta_ref.at[:, cut(whose), :], tab_ref.at[:, :, here]),
-        (lambda whose: spin_ref, w_ref.at[:, here]),
+        (lambda whose: spin_ref, w_ref.at[:, :, here]),
     )
     near = [pltpu.make_async_copy(src(phi), dst, near_sem.at[k]) for k, (src, dst) in enumerate(pieces)]
     far = [
@@ -177,11 +178,17 @@
 
     barrier = pltpu.get_barrier_semaphore()
 
-    def greet(i, _):
+    def greet(i):
         pl.semaphore_signal(barrier, inc=1, device_id=peer(i)[1], device_id_type=MESH)
-        return 0
-
-    lax.fori_loop(1, n, greet, 0)
+
+    def greet_some(step, _):
+        for k in range(7):
+            greet(1 + step * 7 + k)
+        return 0
+
+    lax.fori_loop(0, (n - 1) // 7, greet_some, 0)
+    for k in range(1 + (n - 1) // 7 * 7, n):
+        greet(k)
     pl.semaphore_wait(barrier, n - 1)
     for copy in far:
         copy.start()
@@ -194,16 +201,6 @@
     bound_ref[...] = bound
     bounds_ref[0] = bound
     shrink = 1.0 / bound
-
-    def tell(i):
-        return pltpu.make_async_remote_copy(
-            src_ref=bound_ref,
-            dst_ref=bounds_ref.at[i],
-            send_sem=bsem,
-            recv_sem=brsem,
-            device_id=peer(i)[1],
-            device_id_type=MESH,
-        )
 
     def encoded(dest, target, slot):
         for part in range(share // 16):
@@ -215,49 +212,73 @@
             target[slot, 16 * part : 16 * part + 16, :] = code.astype(I16)
 
     def post(i):
+        where = peer(i)[1]
+        pltpu.make_async_remote_copy(
+            src_ref=bound_ref,
+            dst_ref=bounds_ref.at[i],
+            send_sem=bsem,
+            recv_sem=brsem,
+            device_id=where,
+            device_id_type=MESH,
+        ).start()
         pltpu.make_async_remote_copy(
             src_ref=send_ref.at[i],
             dst_ref=recv_ref.at[i],
             send_sem=ssem,
             recv_sem=rsem.at[i // GROUP],
-            device_id=peer(i)[1],
+            device_id=where,
             device_id_type=MESH,
         ).start()
 
-    def tell_all(i, _):
-        tell(i).start()
-        return 0
-
-    lax.fori_loop(1, n, tell_all, 0)
-    encoded(peer(1)[0], send_ref, 1)
-
-    def ship(i, _):
-        post(i - 1)
+    def fill(i):
         encoded(peer(i)[0], send_ref, i)
-        return 0
-
-    lax.fori_loop(2, n, ship, 0)
+
+    middle = n // 2
+    fill(middle)
+    fill(1)
+    fill(middle + 1)
+    post(middle)
+
+    def ship(step, _):
+        base = 2 + step * UNROLL
+        for k in range(UNROLL):
+            i = base + k
+            post(i - 1)
+            post(middle + i - 1)
+            fill(i)
+            fill(middle + i)
+        return 0
+
+    lax.fori_loop(0, (middle - 2) // UNROLL, ship, 0)
+    post(middle - 1)
+    post(n - 1)
     encoded(me, recv_ref, 0)
-    post(n - 1)
 
     for copy in near[1:]:
         copy.wait()
     for copy in far[1:]:
         copy.wait()
-    degrees = tab_ref.shape[0]
+    degrees, length = tab_ref.shape[0], tab_ref.shape[2]
 
     def arrange(kh, _):
         lanes = pl.ds(pl.multiple_of(kh * LANES, LANES), LANES)
         for j in range(degrees):
             rows = pl.ds(pl.multiple_of(kh * LANES + j * share, share), share)
             t_ref[rows, :] = tab_ref[j, :, lanes].astype(F32)
-        wt_ref[pl.ds(pl.multiple_of(kh * 8, 8), 8), :] = w_ref[:, lanes]
+        w = jnp.concatenate([w_ref[f, :, lanes].astype(F32) for f in range(2)], 0)
+        place = kh * LANES + lax.broadcasted_iota(jnp.int32, w.shape, 1)
+        freq = jnp.where(place < length // 2, place, place - length)
+        row = lax.broadcasted_iota(jnp.int32, w.shape, 0) % degrees
+        ell = jnp.zeros(w.shape, jnp.int32)
+        for j in range(degrees):
+            ell = jnp.where(row == j, ell_ref[j], ell)
+        wt_ref[pl.ds(pl.multiple_of(kh * 8, 8), 8), :] = jnp.where(jnp.abs(freq) <= ell, w, 0.0)
         return 0
 
     lax.fori_loop(0, SPLIT, arrange, 0)
 
     def order(i, _):
-        mine_ref[pl.ds(i, 1), :] = wide_ref[pl.ds(lax.rem(me - i + n, n), 1), :]
+        mine_ref[pl.ds(i, 1), :] = wide_ref[pl.ds((me - i + n) % n, 1), :]
         return 0
 
     lax.fori_loop(0, n, order, 0)
@@ -301,7 +322,8 @@
     )
     bounds.wait_send()
     bounds.wait_recv()
-    for group in range(n // GROUP):
+    groups = n // GROUP
+    for group in [k // 2 + k % 2 * (groups // 2) for k in range(groups)]:
         begin = group * GROUP
         part = pl.ds(max(begin, 1), GROUP - (begin == 0))
         pltpu.make_async_remote_copy(
@@ -338,7 +360,7 @@
     total = jnp.sum(acc_ref[...].reshape(2 * LANES, 8, LANES), 1)
     a_h, a_m = split2(total)
     a_l = (total - a_h.astype(F32) - a_m.astype(F32)).astype(BF16)
-    o_ref[...] = mm(a_h, sum_ref[...]) + mm(a_m, sum_ref[...]) + mm(a_l, sum_ref[...])
+    o_ref[...] = mm(sum_ref[...], a_h, NT) + mm(sum_ref[...], a_m, NT) + mm(sum_ref[...], a_l, NT)
     sent = pl.ds(1, n - 1)
     pltpu.make_async_remote_copy(
         src_ref=send_ref.at[sent],
@@ -350,15 +372,15 @@
     ).wait_send()
 
 
-def sums_of(maps, deltas, spins, position, n):
+def sums_of(maps, deltas, spins, position, ell_index, n):
     degrees, slots, half = deltas.shape
     share = slots * half // position.shape[0]
     length = position.shape[0]
     dma = pltpu.SemaphoreType.DMA
     return pl.pallas_call(
         kernel,
-        out_shape=jax.ShapeDtypeStruct((2 * LANES, LANES), F32),
-        in_specs=[ANY] * 3 + [SMEM] + [VMEM] * 9,
+        out_shape=jax.ShapeDtypeStruct((8, 2 * LANES), F32),
+        in_specs=[ANY] * 3 + [SMEM, SMEM] + [VMEM] * 9,
         out_specs=VMEM,
         scratch_shapes=[
             pltpu.VMEM((4, SPLIT, length), BF16),
@@ -370,7 +392,7 @@
             pltpu.VMEM((1, LANES), F32),
             pltpu.VMEM((n, 1, LANES), F32),
             pltpu.VMEM((degrees, share, length), BF16),
-            pltpu.VMEM((2 * degrees, length), F32),
+            pltpu.VMEM((2, degrees, length), BF16),
             pltpu.VMEM((length, LANES), F32),
             pltpu.VMEM((SPLIT * 2 * degrees, LANES), F32),
             pltpu.VMEM((n, 2 * LANES), F32),
@@ -389,7 +411,7 @@
             collective_id=0, has_side_effects=True, vmem_limit_bytes=56 * 2**20
         ),
         name="coefficient_sums",
-    )(maps, deltas, spins, position, *tables())
+    )(maps, deltas, spins, position, ell_index, *tables())
 
 
 def on_device(maps, deltas, spin_rows, ell_index, owner_map, prior):
@@ -400,16 +422,12 @@
     n = thetas * phis
     degrees = deltas.shape[1]
     share = deltas.shape[2] // phis
-    position = (owner_map % SPLIT) * LANES + owner_map // SPLIT
-    place = phi * half + jnp.arange(half, dtype=jnp.int32)
-    freq = jnp.where(place < length // 2, place, place - length)
-    keep = jnp.abs(freq)[None, None, :] <= ell_index[None, :, None]
-    spins = jnp.where(keep, spin_rows.transpose(1, 2, 0).astype(F32), 0.0).reshape(2 * degrees, half)
-    sums = sums_of(maps, deltas.transpose(1, 2, 0), spins, position, n)
-
-    sums = sums[:, :4].reshape(2, degrees, share, 4).transpose(0, 3, 1, 2)
-    scalar_real, scalar_imag = sums[0, 0] - sums[1, 2], sums[0, 2] + sums[1, 0]
-    spin_real, spin_imag = sums[0, 1] - sums[1, 3], sums[0, 3] + sums[1, 1]
+    position = (owner_map & (SPLIT - 1)) * LANES + owner_map // SPLIT
+    sums = sums_of(maps, deltas.transpose(1, 2, 0), spin_rows.transpose(1, 2, 0), position, ell_index, n)
+
+    sums = sums[:4].reshape(4, 2, degrees, share)
+    scalar_real, scalar_imag = sums[0, 0] - sums[2, 1], sums[2, 0] + sums[0, 1]
+    spin_real, spin_imag = sums[1, 0] - sums[3, 1], sums[3, 0] + sums[1, 1]
     ids = lax.dynamic_slice_in_dim(owner_map, (theta * phis + phi) * share, share)
     slot_freq = jnp.where(ids < length // 2, ids, ids - length)
     ell = ell_index.astype(F32)

time: 109 us -> 104 us (0.954)
  Pallas kernels: 104 us -> 99.3 us
    pallas_call x1, Pallas kernels: 104 us -> 99.3 us  [sums_of(): pl.pallas_call(kernel, out_shape=jax.ShapeDtypeStruct((8, 2 * LANES), F32...]
    reshape x2 -> x1, local copies, waits for them, and re-layouts: 1.65 us -> 0.08 us  [on_device(): sums = sums[:4].reshape(4, 2, degrees, share)]
where the time goes in v2:
time: 104 us; the launch traced here: 103 us
  Pallas kernels  99.3 us (95%)
  local copies, waits for them, and re-layouts  3.28 us (3%)
    pallas_call x1, Pallas kernels, sums_of(): pl.pallas_call(kernel, out_shape=jax.ShapeDtypeStruct((8, 2 * LANES), F32...  99.3 us

profile of v2, /device:TPU:33, one launch (start us, length us, event | category | flops | bytes accessed | tf_op | source)
XLA Modules:
  0.0 103.4 jit_solution(10033071585605065411)
XLA Ops:
  0.0 0.0 copy-start
  0.0 0.7 copy-done
  0.7 0.1 compare_select_fusion.6
  0.8 0.0 copy-start.1
  0.8 0.0 copy-start.3
  0.8 0.6 copy-done.1
  1.5 0.0 copy-done.3
  1.5 0.6 fusion.1.pos_ref
  2.1 99.3 %coefficient_sums.1 = f32[8,256]{1,0:T(8,128)} custom-call(bf16[4,64,2048]{2,1,0:T(8,128)(2,1)} %maps_ref.1, bf16[4,64,2048]{2,1,0:T(8,128)(2,1)} %bitcast.30, bf16[2,4,2048]{2,1,0:T(4,128)(2,1)} %bitcast.31, s32[4096]{0:T(1024)} %fusion.1.pos_ref, s32[4]{0:T(128)} %ell_ref.1, bf16[512,256]{1,0:T(8,128)(2,1)} %constant.96.clone.sh_ref, ...), custom_call_target="tpu_custom_call" | custom-call | tf_op jit(solution)/shard_map/coefficient_sums/pallas_call | solution.py:380
  101.4 0.0 slice-start
  101.4 0.7 slice-done
  102.1 0.0 copy-start.2
  102.1 0.1 reshape.389
  102.2 0.6 copy-done.2
  102.7 0.1 multiply_subtract_fusion
  102.8 0.6 copy.17
  (5 shorter events, 0.0 us)
Async XLA Ops:
  0.0 0.7 copy-start
  0.8 0.7 copy-start.1
  0.8 0.7 copy-start.3
  101.4 0.7 slice-start
  102.1 0.7 copy-start.2

commit v3 on v2

--- a/solution.py
+++ b/solution.py
@@ -140,7 +140,7 @@
     maps_ref, delta_ref, spin_ref, pos_ref, ell_ref, sh_ref, sl_ref, tw_ref, wh_ref, wl_ref, wide_ref, fold_ref, st_ref, sum_ref,
     o_ref,
     x_ref, yh_ref, yl_ref, rt_ref, send_ref, recv_ref, bound_ref, bounds_ref, tab_ref, w_ref, t_ref, wt_ref,
-    mine_ref, h_ref, d_ref, acc_ref, near_sem, far_sem, out_sem, ssem, rsem, bsem, brsem,
+    mine_ref, mh_ref, ml_ref, h_ref, d_ref, acc_ref, near_sem, far_sem, out_sem, ssem, rsem, bsem, brsem,
 ):
     theta, phi = lax.axis_index("theta"), lax.axis_index("phi")
     phis = lax.axis_size("phi")
@@ -282,6 +282,7 @@
         return 0
 
     lax.fori_loop(0, n, order, 0)
+    mh_ref[...], ml_ref[...] = split2(mine_ref[...])
     lane_id = lax.broadcasted_iota(jnp.int32, (1, LANES), 1)
     first = lane_id < HALF
     sign = jnp.where(first, 1.0, -1.0).astype(F32)
@@ -298,8 +299,7 @@
             tops.append(v * st_ref[0] + pltpu.roll(v, HALF, 1) * st_ref[1])
         lows = [pltpu.roll(u, HALF, 1) * sign for u in tops]
         r_h, r_l = split2(jnp.concatenate([jnp.concatenate(tops, 1), jnp.concatenate(lows, 1)], 0))
-        m_h, m_l = split2(mine_ref[...])
-        out = mm3(m_h, m_l, r_h, r_l)
+        out = mm3(mh_ref[...], ml_ref[...], r_h, r_l)
         for i in range(2):
             g = out[:, i * LANES : (i + 1) * LANES]
             back = pltpu.roll(g, HALF, 1)
@@ -308,7 +308,12 @@
             h_ref[rows, LANES:] = jnp.where(first, back, g)
         return 0
 
-    lax.fori_loop(0, LANES // 2, fold, 0)
+    def fold_two(step, _):
+        fold(2 * step, 0)
+        fold(2 * step + 1, 0)
+        return 0
+
+    lax.fori_loop(0, LANES // 4, fold_two, 0)
     acc_ref[...] = jnp.zeros_like(acc_ref)
 
     rest = pl.ds(1, n - 1)
@@ -396,6 +401,8 @@
             pltpu.VMEM((length, LANES), F32),
             pltpu.VMEM((SPLIT * 2 * degrees, LANES), F32),
             pltpu.VMEM((n, 2 * LANES), F32),
+            pltpu.VMEM((n, 2 * LANES), BF16),
+            pltpu.VMEM((n, 2 * LANES), BF16),
             pltpu.VMEM((LANES * LANES, 2 * LANES), F32),
             pltpu.VMEM((GROUP * share, LANES), F32),
             pltpu.VMEM((2 * LANES * 8, LANES), F32),

time: 104 us -> 104 us (level)
  no operation moved by 1% of the time
where the time goes in v3:
time: 104 us; the launch traced here: 103 us
  Pallas kernels  99.3 us (95%)
  local copies, waits for them, and re-layouts  3.28 us (3%)
    pallas_call x1, Pallas kernels, sums_of(): pl.pallas_call(kernel, out_shape=jax.ShapeDtypeStruct((8, 2 * LANES), F32...  99.3 us

profile of v3, /device:TPU:33, one launch (start us, length us, event | category | flops | bytes accessed | tf_op | source)
XLA Modules:
  0.0 103.4 jit_solution(18204781178221712335)
XLA Ops:
  0.0 0.0 copy-start
  0.0 0.7 copy-done
  0.7 0.1 compare_select_fusion.6
  0.8 0.0 copy-start.1
  0.8 0.0 copy-start.3
  0.8 0.6 copy-done.1
  1.5 0.0 copy-done.3
  1.5 0.6 fusion.1.pos_ref
  2.1 99.3 %coefficient_sums.1 = f32[8,256]{1,0:T(8,128)} custom-call(bf16[4,64,2048]{2,1,0:T(8,128)(2,1)} %maps_ref.1, bf16[4,64,2048]{2,1,0:T(8,128)(2,1)} %bitcast.30, bf16[2,4,2048]{2,1,0:T(4,128)(2,1)} %bitcast.31, s32[4096]{0:T(1024)} %fusion.1.pos_ref, s32[4]{0:T(128)} %ell_ref.1, bf16[512,256]{1,0:T(8,128)(2,1)} %constant.96.clone.sh_ref, ...), custom_call_target="tpu_custom_call" | custom-call | tf_op jit(solution)/shard_map/coefficient_sums/pallas_call | solution.py:385
  101.4 0.0 slice-start
  101.4 0.7 slice-done
  102.1 0.0 copy-start.2
  102.1 0.1 reshape.389
  102.1 0.6 copy-done.2
  102.7 0.1 multiply_subtract_fusion
  102.8 0.6 copy.17
  (5 shorter events, 0.0 us)
Async XLA Ops:
  0.0 0.7 copy-start
  0.8 0.7 copy-start.1
  0.8 0.7 copy-start.3
  101.4 0.7 slice-start
  102.1 0.7 copy-start.2
